TPU v7x, 32 devices: a whole 2x2x4 slice. The times are simulated.
32 devices in a mesh: dp: 8 (over y, x, core), mp: 4 (over z).
Axes of the slice: x: 2, y: 2, z: 4, core: 2. Of those that a mesh axis runs over, the one named last changes fastest.
Arguments:
- states: bfloat16 [128, 80, 768], P('dp'), may hold values from -6 to 6
- hist_len: int32 [128], P('dp'), may hold values from 1 to 20
- norm_gain: float32 [768], replicated, may hold values from 0.5 to 1.5
- qkv_weight: bfloat16 [768, 3, 12, 64], P(None, None, 'mp'), may hold values from -1 to 1
- output_weight: bfloat16 [12, 64, 768], P('mp'), may hold values from -0.21875 to 0.21875
- cotangent: bfloat16 [128, 80, 768], P('dp'), may hold values from -6 to 6
Outputs:
- attended: bfloat16 [128, 80, 768], P('dp')
- grad_states: bfloat16 [128, 80, 768], P('dp')
- grad_qkv: float32 [768, 3, 12, 64], P('dp', None, 'mp')
- output_weight_gradient: float32 [12, 64, 768], P('mp', None, 'dp')
- grad_gain: float32 [768], P('dp')
All inputs are finite; a program needn't handle non-finite values.
Results may differ from a plain program's by a relative error of at most 0.012.
Values may be sent and summed in bfloat16 or wider, within the bound.
A program may use at most 128 MiB of HBM per device.

v0:
```python
import functools

import jax
import jax.numpy as jnp
from jax import lax
from jax.experimental import pallas as pl
from jax.experimental.pallas import tpu as pltpu
from jax.sharding import PartitionSpec as P

LEVELS = 4
PIECES = 16
GROUP = 4
PACK = 2
BF = jnp.bfloat16
F32 = jnp.float32
MESH = pl.DeviceIdType.MESH


def dot(a, b, ca, cb):
    return lax.dot_general(a, b, (((ca,), (cb,)), ((), ())), preferred_element_type=F32)


def remote(src, dst, ssem, rsem, device):
    return pltpu.make_async_remote_copy(
        src_ref=src, dst_ref=dst, send_sem=ssem, recv_sem=rsem, device_id=device, device_id_type=MESH
    )


def gather_kernel(n, own, wall, s_z, r_z, s_x, r_x, s_d, r_d, s_c, r_c):
    d, z = lax.axis_index("dp"), lax.axis_index("mp")
    c, bx, by = d % 2, (d // 2) % 2, (d // 4) % 2
    partner = (d + 1 - 2 * c, z)
    across = ((d + 2 - 4 * bx, z), (d + 4 - 8 * by, z))
    barrier = pltpu.get_barrier_semaphore()
    greet = [(d, (z + n - j) % n) for j in range(1, n)] + list(across) + [partner]
    for device in greet:
        pl.semaphore_signal(barrier, inc=1, device_id=device, device_id_type=MESH)
    pl.semaphore_wait(barrier, len(greet))

    def place(x, y, core):
        return 4 * (x + 2 * y) + 2 * core

    mine = place(bx, by, c)
    sides = (place(1 - bx, by, c), place(bx, 1 - by, c))
    diag = place(1 - bx, 1 - by, c)
    order = [j for j in (1, n - 1) if j < n] + [j for j in range(2, n - 1)]
    sends = []

    def go(src, dst, ssem, rsem, device):
        copy = remote(src, dst, ssem, rsem, device)
        copy.start()
        sends.append(copy)

    def arrived(spot, rsem):
        remote(spot, spot, rsem, rsem, partner).wait_recv()

    for j in order:
        go(own.at[pl.ds(mine, 2)], wall.at[j - 1, pl.ds(mine, 2)], s_z.at[j - 1], r_z.at[j - 1], (d, (z + n - j) % n))
    for j in order:
        spot = wall.at[j - 1, pl.ds(mine, 2)]
        arrived(spot, r_z.at[j - 1])
        for i in range(2):
            go(spot, spot, s_x.at[i, j - 1], r_x.at[i, j - 1], across[i])
        go(spot, spot, s_c.at[0, j - 1], r_c.at[0, j - 1], partner)
    for j in order:
        for i in range(2):
            spot = wall.at[j - 1, pl.ds(sides[i], 2)]
            arrived(spot, r_x.at[i, j - 1])
            piece = wall.at[j - 1, sides[i] + i]
            go(piece, piece, s_d.at[i, j - 1], r_d.at[i, j - 1], across[1 - i])
            go(spot, spot, s_c.at[1 + i, j - 1], r_c.at[1 + i, j - 1], partner)
    for j in order:
        for i in range(2):
            piece = wall.at[j - 1, diag + i]
            arrived(piece, r_d.at[i, j - 1])
            go(piece, piece, s_c.at[3 + i, j - 1], r_c.at[3 + i, j - 1], partner)
    flip = 2 - 4 * c
    for j in order:
        for k, spot in enumerate((mine, sides[0], sides[1])):
            arrived(wall.at[j - 1, pl.ds(spot + flip, 2)], r_c.at[k, j - 1])
        for i in range(2):
            arrived(wall.at[j - 1, diag + i + flip], r_c.at[3 + i, j - 1])
    for copy in sends:
        copy.wait_send()


def gather(own, n):
    one, two, five = (pltpu.SemaphoreType.DMA(k + (n - 1,)) for k in ((), (2,), (5,)))
    return pl.pallas_call(
        functools.partial(gather_kernel, n),
        out_shape=jax.ShapeDtypeStruct((n - 1,) + own.shape, own.dtype),
        in_specs=[pl.BlockSpec(memory_space=pl.ANY)],
        out_specs=pl.BlockSpec(memory_space=pl.ANY),
        scratch_shapes=[one, one, two, two, two, two, five, five],
        compiler_params=pltpu.CompilerParams(collective_id=1, has_side_effects=True),
        name="gather",
    )(own)


def scatter_kernel(half, part, out, got, total, held, s_c, r_c, s_o, r_o):
    d, z = lax.axis_index("dp"), lax.axis_index("mp")
    c, chip = d % 2, d // 2
    partner = (d + 1 - 2 * c, z)
    others = [(((chip + o) % half) * 2 + c, z) for o in range(1, half)]
    barrier = pltpu.get_barrier_semaphore()
    for device in others + [partner]:
        pl.semaphore_signal(barrier, inc=1, device_id=device, device_id_type=MESH)
    pl.semaphore_wait(barrier, half)
    order = list(range(1, half)) + [0]
    sends = []
    for o in order:
        t = (chip + o) % half
        copy = remote(part.at[1 - c, t], got.at[o], s_c.at[o], r_c.at[o], partner)
        copy.start()
        sends.append(copy)
    for o in order:
        t = (chip + o) % half
        remote(got.at[o], got.at[o], s_c.at[o], r_c.at[o], partner).wait_recv()
        both = part[c, t].astype(F32) + got[o].astype(F32)
        if o == 0:
            out[...] = both
        else:
            total[o - 1] = both.astype(BF)
            copy = remote(total.at[o - 1], held.at[o - 1], s_o.at[o - 1], r_o.at[o - 1], others[o - 1])
            copy.start()
            sends.append(copy)
    for o in range(1, half):
        remote(held.at[o - 1], held.at[o - 1], s_o.at[o - 1], r_o.at[o - 1], partner).wait_recv()
        out[...] += held[o - 1].astype(F32)
    for copy in sends:
        copy.wait_send()


def scatter(part):
    _, half, rows, wide = part.shape
    return pl.pallas_call(
        functools.partial(scatter_kernel, half),
        out_shape=jax.ShapeDtypeStruct((rows, wide), F32),
        in_specs=[pl.BlockSpec(memory_space=pltpu.VMEM)],
        out_specs=pl.BlockSpec(memory_space=pltpu.VMEM),
        scratch_shapes=[
            pltpu.VMEM((half, rows, wide), BF),
            pltpu.VMEM((half - 1, rows, wide), BF),
            pltpu.VMEM((half - 1, rows, wide), BF),
            pltpu.SemaphoreType.DMA((half,)),
            pltpu.SemaphoreType.DMA((half,)),
            pltpu.SemaphoreType.DMA((half - 1,)),
            pltpu.SemaphoreType.DMA((half - 1,)),
        ],
        compiler_params=pltpu.CompilerParams(collective_id=2, has_side_effects=True),
        name="scatter",
    )(part)


def work_kernel(nb, n, width, hist, states, cot, gain, own, wall, att, gst, part,
                wq, wo, acc, gacc, proj, gproj, ctx, gctx, sems):
    i = pl.program_id(0)
    _, s, dim = states.shape
    rows = nb * s
    lanes = GROUP * 64

    @pl.when(i == 0)
    def _():
        copies = []
        for j in range(n):
            src = own if j == 0 else wall.at[j - 1]
            for k in range(4):
                at = pl.ds(k * width, width)
                dst = wo.at[pl.ds(j * width, width)] if k == 3 else wq.at[pl.ds(k * n * width + j * width, width)]
                copies.append(pltpu.make_async_copy(src.at[at], dst, sems.at[j, k]))
        for copy in copies:
            copy.start()
        acc[...] = jnp.zeros_like(acc)
        gacc[...] = jnp.zeros_like(gacc)
        for copy in copies:
            copy.wait()

    wide = states[...].reshape(rows, dim).astype(F32)
    inv = lax.rsqrt(jnp.mean(wide * wide, axis=-1, keepdims=True) + 1e-06)
    unit = wide * inv
    normed = (unit * gain[...]).astype(BF)
    for k in range(3):
        cols = pl.ds(k * dim, dim)
        proj[:, cols] = dot(normed, wq[cols, :], 1, 1).astype(BF)
    pos = lax.broadcasted_iota(jnp.int32, (s, dim), 0)
    mcot = jnp.concatenate(
        [jnp.where(pos < LEVELS * hist[i * nb + b], cot[b].astype(F32), 0.0) for b in range(nb)], axis=0
    ).astype(BF)
    gctx[...] = dot(mcot, wo[...], 1, 1).astype(BF)

    pack = PACK * 64
    lane = lax.broadcasted_iota(jnp.int32, (s, pack), 1) // 64
    key_pos = lax.broadcasted_iota(jnp.int32, (PACK, s, s), 1)

    only = [(lane == h).astype(F32).astype(BF) for h in range(PACK)]

    def spread(x):
        return jnp.concatenate([x * only[h] for h in range(PACK)], axis=0)

    def fold(x):
        out = x[(PACK - 1) * s :]
        for h in range(PACK - 1):
            out = jnp.where(lane == h, x[h * s : (h + 1) * s], out)
        return out.astype(BF)

    @pl.loop(0, nb, unroll=4)
    def _(b):
        at = pl.ds(pl.multiple_of(b * s, 16), s)
        keep = key_pos < LEVELS * hist[i * nb + b]
        for g in range(dim // pack):
            cols = [pl.ds(k * dim + g * pack, pack) for k in range(3)]
            here = pl.ds(g * pack, pack)
            q, gc = proj[at, cols[0]], gctx[at, here]
            kk, vv = spread(proj[at, cols[1]]), spread(proj[at, cols[2]])
            sc = dot(kk, q, 1, 1).reshape(PACK, s, s)
            sc = jnp.where(keep, sc, -1e30)
            ex = jnp.exp(sc - jnp.max(sc, axis=1, keepdims=True))
            prob = ex * (1.0 / jnp.sum(ex, axis=1, keepdims=True))
            pb = prob.reshape(PACK * s, s).astype(BF)
            ctx[at, here] = dot(pb, vv, 0, 0).astype(BF)
            gp = dot(vv, gc, 1, 1).reshape(PACK, s, s)
            delta = jnp.sum(prob * gp, axis=1, keepdims=True)
            ds = (prob * (gp - delta)).reshape(PACK * s, s).astype(BF)
            gproj[at, cols[0]] = dot(ds, kk, 0, 0).astype(BF)
            gproj[at, cols[1]] = fold(dot(ds, q, 1, 0))
            gproj[at, cols[2]] = fold(dot(pb, gc, 1, 0))

    att[...] = (wide + dot(ctx[...], wo[...], 1, 0)).astype(BF).reshape(nb, s, dim)
    gn = dot(gproj[...], wq[...], 1, 0)
    for k in range(3):
        acc[:, k * lanes : (k + 1) * lanes] += dot(normed, gproj[:, k * dim : k * dim + lanes], 0, 0)
    acc[:, 3 * lanes :] += dot(mcot, ctx[:, :lanes], 0, 0)
    gacc[...] += jnp.sum((gn * unit).reshape(rows // 8, 8, dim), axis=0)
    gu = gn * gain[...]
    corr = jnp.mean(gu * unit, axis=-1, keepdims=True)
    gst[...] = (mcot.astype(F32) + inv * (gu - unit * corr)).astype(BF).reshape(nb, s, dim)

    @pl.when(i == pl.num_programs(0) - 1)
    def _():
        total = jnp.sum(gacc[...], axis=0, keepdims=True)
        column = jnp.broadcast_to(total, (128, dim)).T
        high = column.astype(BF).astype(F32)
        at = lax.broadcasted_iota(jnp.int32, (dim, 128), 1)
        last = slice(4 * lanes - 128, 4 * lanes)
        acc[:, last] = jnp.where(at < 64, acc[:, last], jnp.where(at < 96, high, column - high))
        _, half, piece, _ = part.shape
        for t in range(2 * half):
            part[t % 2, t // 2] = acc[t * piece : (t + 1) * piece, :].astype(BF)


def work(states, hist, gain, own, wall, cot, n, nd):
    count, s, dim = states.shape
    nb = 4 if count % 4 == 0 else 1
    rows, lanes = nb * s, GROUP * 64
    width = dim // n
    block = pl.BlockSpec((nb, s, dim), lambda i, *_: (i, 0, 0))
    piece = (2, nd // 2, dim // nd, 4 * lanes)
    return pl.pallas_call(
        functools.partial(work_kernel, nb, n, width),
        out_shape=(
            jax.ShapeDtypeStruct(states.shape, BF),
            jax.ShapeDtypeStruct(states.shape, BF),
            jax.ShapeDtypeStruct(piece, BF),
        ),
        grid_spec=pltpu.PrefetchScalarGridSpec(
            num_scalar_prefetch=1,
            grid=(count // nb,),
            in_specs=[
                block,
                block,
                pl.BlockSpec((1, dim), lambda i, *_: (0, 0)),
                pl.BlockSpec(memory_space=pl.ANY),
                pl.BlockSpec(memory_space=pl.ANY),
            ],
            out_specs=[block, block, pl.BlockSpec(piece, lambda i, *_: (0, 0, 0, 0))],
            scratch_shapes=[
                pltpu.VMEM((3 * dim, dim), BF),
                pltpu.VMEM((dim, dim), BF),
                pltpu.VMEM((dim, 4 * lanes), F32),
                pltpu.VMEM((8, dim), F32),
                pltpu.VMEM((rows, 3 * dim), BF),
                pltpu.VMEM((rows, 3 * dim), BF),
                pltpu.VMEM((rows, dim), BF),
                pltpu.VMEM((rows, dim), BF),
                pltpu.SemaphoreType.DMA((n, 4)),
            ],
        ),
        compiler_params=pltpu.CompilerParams(
            dimension_semantics=("arbitrary",), vmem_limit_bytes=56 * 1024 * 1024
        ),
        name="work",
    )(hist, states, cot, gain.reshape(1, dim), own, wall)


def body(nd, n, states, hist_len, norm_gain, qkv_weight, output_weight, cotangent):
    dim, _, heads, size = qkv_weight.shape
    width = heads * size
    lanes = GROUP * 64
    own = jnp.concatenate([qkv_weight.reshape(dim, 3 * width).T, output_weight.reshape(width, dim)], axis=0)
    wall = gather(own.reshape(PIECES, 4 * width // PIECES, dim), n).reshape(n - 1, 4 * width, dim)
    attended, grad_states, part = work(states, hist_len, norm_gain, own, wall, cotangent, n, nd)
    summed = scatter(part)
    grads = summed.reshape(dim // nd, 4, lanes)
    grad_qkv = grads[:, :3, :width].reshape(dim // nd, 3, heads, size)
    grad_out = grads[:, 3, :width].T.reshape(heads, size, dim // nd)
    grad_gain = grads[:, 3, 192] + grads[:, 3, 224]
    return attended, grad_states, grad_qkv, grad_out, grad_gain


def solution(mesh):
    placed = (
        P("dp", None, None),
        P("dp"),
        P(),
        P(None, None, "mp", None),
        P("mp", None, None),
        P("dp", None, None),
    )
    return jax.shard_map(
        functools.partial(body, mesh.shape["dp"], mesh.shape["mp"]),
        mesh=mesh,
        in_specs=placed,
        out_specs=(
            P("dp", None, None),
            P("dp", None, None),
            P("dp", None, "mp", None),
            P("mp", None, "dp"),
            P("dp"),
        ),
        check_vma=False,
    )
```

profile of v0, /device:TPU:0, one launch (start us, length us, event | category | flops | bytes accessed | tf_op | source)
XLA Modules:
  0.0 99.5 jit_solution(14173943890482599783)
XLA Ops:
  0.6 1.3 %reshape.35.gain = f32[1,768]{1,0:T(1,128)} reshape(f32[768]{0:T(1024)} %param.8) | data formatting | bytes 6144 | tf_op jit(solution)/shard_map/reshape | solution.py:292
  1.9 2.4 %pad_maximum_fusion.own = bf16[768,768]{1,0:T(8,128)(2,1)} fusion(bf16[192,768]{1,0:T(8,128)(2,1)} %bitcast.20, bf16[576,768]{1,0:T(8,128)(2,1)} %bitcast.19), kind=kLoop, calls=%fused_computation | loop fusion | flops 2359296 | bytes 2359296 | tf_op jit(solution)/shard_map/concatenate | solution.py:299
  4.3 31.5 %gather.1 = bf16[3,16,48,768]{3,2,1,0:T(8,128)(2,1)} custom-call(bf16[16,48,768]{2,1,0:T(8,128)(2,1)} %bitcast.17), custom_call_target="tpu_custom_call" | custom-call | tf_op jit(solution)/shard_map/gather/pallas_call | solution.py:89
  35.8 44.3 %work.1 = (bf16[16,80,768]{2,1,0:T(8,128)(2,1)}, bf16[16,80,768]{2,1,0:T(8,128)(2,1)}, bf16[2,4,96,1024]{3,2,1,0:T(8,128)(2,1)}) custom-call(s32[16]{0:T(128)} %hist.1, bf16[16,80,768]{2,1,0:T(8,128)(2,1)} %states.1, bf16[16,80,768]{2,1,0:T(8,128)(2,1)} %cot.1, f32[1,768]{1,0:T(1,128)} %reshape.35.gain, bf16[768,768]{1,0:T(8,128)(2,1)} %pad_maximum_fusion.own, ...), custom_call_target="tpu_custom_call" | custom-call | tf_op jit(solution)/shard_map/work/pallas_call | solution.py:258
  80.1 15.4 %scatter.1 = f32[96,1024]{1,0:T(8,128)} custom-call(bf16[2,4,96,1024]{3,2,1,0:T(8,128)(2,1)} %get-tuple-element.10.part), custom_call_target="tpu_custom_call" | custom-call | tf_op jit(solution)/shard_map/scatter/pallas_call | solution.py:136
  95.6 1.2 %reshape.40 = f32[96,4,256]{2,1,0:T(4,128)S(1)} reshape(f32[96,1024]{1,0:T(8,128)} %scatter.1) | data formatting | bytes 786432 | tf_op jit(solution)/shard_map/reshape | solution.py:303
  96.8 0.1 slice.17
  96.9 0.7 copy.18
  97.6 0.3 fusion
  97.9 0.1 copy.17
  98.0 0.1 copy.16
  98.0 0.5 add_bitcast_fusion
  98.6 0.9 copy.11
where the time goes:
time: 99.8 us; the launch traced here: 99.5 us
  Pallas kernels  91.3 us (91%)
  local copies, waits for them, and re-layouts  4.6 us (5%)
  other arithmetic  2.92 us (3%)
    pallas_call x1, Pallas kernels, work(): pl.pallas_call(functools.partial(work_kernel, nb, n, width), out_shape=(j...  44.3 us
    pallas_call x1, Pallas kernels, gather(): pl.pallas_call(functools.partial(gather_kernel, n), out_shape=jax.ShapeDt...  31.5 us
    pallas_call x1, Pallas kernels, scatter(): pl.pallas_call(functools.partial(scatter_kernel, half), out_shape=jax.Sha...  15.4 us
    concatenate x1, other arithmetic, body(): jnp.concatenate([qkv_weight.reshape(dim, 3 * width).T, output_weight.resh...  2.39 us

commit v1 on v0

v1 whole, which is shorter than its diff:
```python
import functools

import jax
import jax.numpy as jnp
from jax import lax
from jax.experimental import pallas as pl
from jax.experimental.pallas import tpu as pltpu
from jax.sharding import PartitionSpec as P

LEVELS = 4
NB = 4
WIN = 256
BF = jnp.bfloat16
F32 = jnp.float32
MESH = pl.DeviceIdType.MESH


def dot(a, b, ca, cb):
    return lax.dot_general(a, b, (((ca,), (cb,)), ((), ())), preferred_element_type=F32)


def kernel(n, nd, s, hist, states, cot, gain, wqkv, wout, att, gst, gq, go, gg,
           wall, st, mc, normed, inv, pj, sq, sg, scb, gpb, pbb, dsb, ctx, gproj,
           part, got, total, held, tot, zz, res, gqv, gov, ggv,
           s_w, s_in, s_out, s_res, s_z, r_z, s_x, r_x, s_d, r_d, s_c, r_c, s_p, r_p, s_o, r_o, s_g, r_g):
    rows_all, dim = st.shape
    width = wout.shape[0]
    rows = NB * s
    nblk = rows_all // rows
    half = nd // 2
    piece = dim // nd
    d, z = lax.axis_index("dp"), lax.axis_index("mp")
    c, chip = d % 2, d // 2
    bx, by = chip % 2, (chip // 2) % 2
    partner = (d + 1 - 2 * c, z)
    across = ((d + 2 - 4 * bx, z), (d + 4 - 8 * by, z))
    others = [(((chip + o) % half) * 2 + c, z) for o in range(1, half)]
    zpeers = [(d, (z + n - j) % n) for j in range(1, n)]

    loads = []
    for k in range(3):
        loads.append(pltpu.make_async_copy(
            wqkv.at[pl.ds(k * width, width)], wall.at[pl.ds(k * dim, width)], s_w.at[k]))
    loads.append(pltpu.make_async_copy(wout, wall.at[pl.ds(3 * dim, width)], s_w.at[3]))
    for copy in loads:
        copy.start()
    for i in range(nblk):
        at = pl.ds(i * rows, rows)
        pltpu.make_async_copy(states.at[at], st.at[at], s_in.at[0, i]).start()
        pltpu.make_async_copy(cot.at[at], mc.at[at], s_in.at[1, i]).start()

    barrier = pltpu.get_barrier_semaphore()
    greet = zpeers + others + [partner]
    for device in greet:
        pl.semaphore_signal(barrier, inc=1, device_id=device, device_id_type=MESH)
    pj[...] = jnp.zeros_like(pj)
    sq[...] = jnp.zeros_like(sq)
    sg[...] = jnp.zeros_like(sg)
    for copy in loads:
        copy.wait()
    pl.semaphore_wait(barrier, len(greet))

    def remote(src, dst, ssem, rsem, device):
        return pltpu.make_async_remote_copy(
            src_ref=src, dst_ref=dst, send_sem=ssem, recv_sem=rsem, device_id=device, device_id_type=MESH
        )

    def arrived(spot, rsem):
        remote(spot, spot, rsem, rsem, partner).wait_recv()

    quarter = width // 4

    def spot(j, x, y, core, i=0, count=2):
        first = pl.multiple_of((x + 2 * y) * dim + place[j] * width + (2 * core + i) * quarter, 16)
        return wall.at[pl.ds(first, count * quarter)]

    order = [j for j in (1, n - 1) if j < n] + [j for j in range(2, n - 1)]
    place = {j: m for m, j in enumerate([0] + order)}

    def send_own():
        mine = spot(0, bx, by, c)
        for j in order:
            remote(mine, spot(j, bx, by, c), s_z.at[j - 1], r_z.at[j - 1], zpeers[j - 1]).start()

    def first_hop(j):
        here = spot(j, bx, by, c)
        arrived(here, r_z.at[j - 1])
        for i in range(2):
            remote(here, here, s_x.at[i, j - 1], r_x.at[i, j - 1], across[i]).start()
        remote(here, here, s_c.at[0, j - 1], r_c.at[0, j - 1], partner).start()

    sides = ((1 - bx, by), (bx, 1 - by))
    diag = (1 - bx, 1 - by)

    def second_hop(j):
        for i in range(2):
            here = spot(j, *sides[i], c)
            arrived(here, r_x.at[i, j - 1])
            one = spot(j, *sides[i], c, i, 1)
            remote(one, one, s_d.at[i, j - 1], r_d.at[i, j - 1], across[1 - i]).start()
            remote(here, here, s_c.at[1 + i, j - 1], r_c.at[1 + i, j - 1], partner).start()

    def third_hop(j):
        for i in range(2):
            one = spot(j, *diag, c, i, 1)
            arrived(one, r_d.at[i, j - 1])
            remote(one, one, s_c.at[3 + i, j - 1], r_c.at[3 + i, j - 1], partner).start()

    def landed(j):
        for k, (x, y) in enumerate(((bx, by),) + sides):
            arrived(spot(j, x, y, 1 - c), r_c.at[k, j - 1])
        for i in range(2):
            arrived(spot(j, *diag, 1 - c, i, 1), r_c.at[3 + i, j - 1])

    scatter_order = list(range(1, half)) + [0]

    def scatter_core():
        for o in scatter_order:
            t = (chip + o) % half
            remote(part.at[1 - c, t], got.at[o], s_p.at[o], r_p.at[o], partner).start()

    def scatter_chip():
        for o in scatter_order:
            t = (chip + o) % half
            arrived(got.at[o], r_p.at[o])
            both = part[c, t].astype(F32) + got[o].astype(F32)
            if o == 0:
                tot[:piece, :] = both
            else:
                total[o - 1] = both.astype(BF)
                remote(total.at[o - 1], held.at[o - 1], s_o.at[o - 1], r_o.at[o - 1], others[o - 1]).start()

    def scatter_sum():
        for o in range(1, half):
            arrived(held.at[o - 1], r_o.at[o - 1])
            tot[:piece, :] += held[o - 1].astype(F32)
        column = lax.broadcasted_iota(jnp.int32, (dim, 128), 1)
        row = lax.broadcasted_iota(jnp.int32, (dim, 128), 0)
        pick = (row - piece * d == column).astype(F32).astype(BF)
        gsum = jnp.zeros((1, 128), F32)
        for k in range(4):
            turned = tot[:, k * WIN : (k + 1) * WIN].T[:width]
            if k < 3:
                gqv[k * width : (k + 1) * width, :] = turned[:, :piece]
                mine = dot(wall[k * dim : k * dim + width, :], pick, 1, 0)
                gsum = gsum + jnp.sum(mine * turned, axis=0, keepdims=True)
            else:
                gov[...] = turned[:, :piece]
        scale = gain[...]
        own_gain = jnp.ones((1, piece), F32)
        for t in range(nd):
            own_gain = jnp.where(d == t, scale[:, t * piece : (t + 1) * piece], own_gain)
        zz[z, 0:1, :piece] = gsum[:, :piece] / own_gain
        for j in range(1, n):
            remote(zz.at[z], zz.at[z], s_g.at[j - 1], r_g.at[j - 1], zpeers[j - 1]).start()
        pltpu.make_async_copy(gqv, gq, s_res.at[0]).start()
        pltpu.make_async_copy(gov, go, s_res.at[1]).start()

    def gain_sum():
        for j in range(1, n):
            arrived(zz.at[(z + j) % n], r_g.at[j - 1])
        value = zz[0, 0:1, :piece]
        for k in range(1, n):
            value = value + zz[k, 0:1, :piece]
        ggv[...] = value
        pltpu.make_async_copy(ggv, gg, s_res.at[2]).start()

    lane = lax.broadcasted_iota(jnp.int32, (s, 128), 1)
    low = (lane < 64).astype(F32).astype(BF)
    high = (lane >= 64).astype(F32).astype(BF)
    key_pos = lax.broadcasted_iota(jnp.int32, (s, WIN), 0)

    def spread(x, out, odd):
        left, right = x[:, :128], x[:, 128:]
        if odd:
            out[0:s, :128] = left * high
            out[s : 2 * s, 128:] = right * low
            out[2 * s : 3 * s, 128:] = right * high
        else:
            out[0:s, :128] = left * low
            out[s : 2 * s, :128] = left * high
            out[2 * s : 3 * s, 128:] = right * low

    def fold(x, odd):
        a, b, e = x[:s], x[s : 2 * s], x[2 * s : 3 * s]
        if odd:
            left = jnp.where(lane < 64, 0.0, a[:, :128])
            right = jnp.where(lane < 64, b[:, 128:], e[:, 128:])
        else:
            left = jnp.where(lane < 64, a[:, :128], b[:, :128])
            right = jnp.where(lane < 64, e[:, 128:], 0.0)
        return jnp.concatenate([left, right], axis=1)

    def put(ref, at, base, x, odd):
        x = x.astype(BF)
        if odd:
            ref[at, base + 128 : base + 256] += x[:, :128]
            ref[at, base + 256 : base + 384] = x[:, 128:]
        else:
            ref[at, base : base + 256] = x

    def prepare(i):
        at = pl.ds(pl.multiple_of(i * rows, 16), rows)
        pltpu.make_async_copy(states.at[at], st.at[at], s_in.at[0, i]).wait()
        pltpu.make_async_copy(cot.at[at], mc.at[at], s_in.at[1, i]).wait()
        wide = st[at, :].astype(F32)
        scale = lax.rsqrt(jnp.mean(wide * wide, axis=-1, keepdims=True) + 1e-06)
        inv[at, :] = scale
        normed[at, :] = (wide * scale * gain[...]).astype(BF)
        pos = lax.broadcasted_iota(jnp.int32, (s, dim), 0)
        for b in range(NB):
            one = pl.ds(pl.multiple_of(i * rows + b * s, 16), s)
            keep = pos < LEVELS * hist[i * NB + b]
            mc[one, :] = jnp.where(keep, mc[one, :].astype(F32), 0.0).astype(BF)

    def attention(slot, i):
        odd = slot % 2
        base = 2 * width * (slot // 2)
        first = slot * width - 64 * odd
        cols = width + 64 * odd
        at = pl.ds(pl.multiple_of(i * rows, 16), rows)
        for k in range(4):
            lhs = normed[at, :] if k < 3 else mc[at, :]
            pj[k, :, :cols] = dot(lhs, wall[k * dim + first : k * dim + first + cols, :], 1, 1).astype(BF)

        def scores(b):
            mine = slice(b * s, (b + 1) * s)
            spread(pj[0, mine, :], sq.at[odd, b], odd)
            spread(pj[3, mine, :], sg.at[odd, b], odd)
            scb[b] = dot(pj[1, mine, :], sq[odd, b], 1, 1)
            gpb[b] = dot(pj[2, mine, :], sg[odd, b], 1, 1)

        def soft(b):
            keep = key_pos < LEVELS * hist[i * NB + b]
            sc = jnp.where(keep, scb[b], -1e30)
            ex = jnp.exp(sc - jnp.max(sc, axis=0, keepdims=True))
            prob = ex * (1.0 / jnp.sum(ex, axis=0, keepdims=True))
            pbb[b] = prob.astype(BF)
            gp = gpb[b]
            delta = jnp.sum(prob * gp, axis=0, keepdims=True)
            dsb[b] = (prob * (gp - delta)).astype(BF)

        def outs(b):
            mine = slice(b * s, (b + 1) * s)
            one = pl.ds(pl.multiple_of(i * rows + b * s, 16), s)
            pb, ds = pbb[b], dsb[b]
            put(gproj, one, dim + base, dot(ds, sq[odd, b], 1, 0), odd)
            put(gproj, one, 2 * dim + base, dot(pb, sg[odd, b], 1, 0), odd)
            put(ctx, one, base, fold(dot(pb, pj[2, mine, :], 0, 0), odd), odd)
            put(gproj, one, base, fold(dot(ds, pj[1, mine, :], 0, 0), odd), odd)

        scores(0)
        scores(1)
        for b in range(NB):
            soft(b)
            if b + 2 < NB:
                scores(b + 2)
            outs(b)

    def weight_grads():
        for k in range(4):
            lhs = normed[...] if k < 3 else mc[...]
            rhs = gproj[:, k * dim : k * dim + WIN] if k < 3 else ctx[:, :WIN]
            acc = dot(lhs, rhs, 0, 0)
            for t in range(nd):
                part[t % 2, t // 2, :, k * WIN : (k + 1) * WIN] = acc[t * piece : (t + 1) * piece].astype(BF)

    def results(i):
        at = pl.ds(pl.multiple_of(i * rows, 16), rows)
        wide = st[at, :].astype(F32)
        copies = [
            pltpu.make_async_copy(res.at[k, i % 2], (att, gst)[k].at[at], s_out.at[k, i % 2]) for k in range(2)
        ]

        @pl.when(i >= 2)
        def _():
            for copy in copies:
                copy.wait()

        res[0, i % 2] = (wide + dot(ctx[at, :], wall[3 * dim :, :], 1, 0)).astype(BF)
        gn = dot(gproj[at, :], wall[: 3 * dim, :], 1, 0)
        scale = inv[at, :]
        unit = wide * scale
        gu = gn * gain[...]
        corr = jnp.mean(gu * unit, axis=-1, keepdims=True)
        res[1, i % 2] = (mc[at, :].astype(F32) + scale * (gu - unit * corr)).astype(BF)
        for copy in copies:
            copy.start()

    def at_step(i, steps):
        for k, step in enumerate(steps):
            if step:
                @pl.when(i == k)
                def _():
                    for one in step:
                        one()

    plan = {stage: [[] for _ in range(nblk)] for stage in range(n)}

    def note(stage, i, step, *args):
        spots = [(a, b) for a in range(n) for b in range(nblk)]
        place = min(stage * nblk + i, len(spots) - 1)
        a, b = spots[place]
        plan[a][b].append(functools.partial(step, *args))

    tail = []
    for m, j in enumerate(order):
        begin = m * nblk
        note(0, begin + 1, first_hop, j)
        note(0, begin + 2, second_hop, j)
        note(0, begin + 3, third_hop, j)
        plan[m + 1][0].insert(0, functools.partial(landed, j))
    note(1, 1, scatter_chip)
    note(2, 1, scatter_sum)
    note(3, 1, gain_sum)

    send_own()
    for m in range(n):
        @pl.loop(0, nblk)
        def _(i):
            at_step(i, plan[m])
            if m == 0:
                prepare(i)
            attention(m, i)
        if m == 0:
            weight_grads()
            scatter_core()

    pl.loop(0, nblk)(results)

    for i in range(max(nblk - 2, 0), nblk):
        at = pl.ds(i * rows, rows)
        for k in range(2):
            pltpu.make_async_copy(res.at[k, i % 2], (att, gst)[k].at[at], s_out.at[k, i % 2]).wait()
    pltpu.make_async_copy(gqv, gq, s_res.at[0]).wait()
    pltpu.make_async_copy(gov, go, s_res.at[1]).wait()
    pltpu.make_async_copy(ggv, gg, s_res.at[2]).wait()

    def sent(src, ssem):
        remote(src, src, ssem, ssem, partner).wait_send()

    for j in order:
        here = spot(j, bx, by, c)
        sent(here, s_z.at[j - 1])
        sent(here, s_c.at[0, j - 1])
        for i in range(2):
            sent(here, s_x.at[i, j - 1])
            sent(here, s_c.at[1 + i, j - 1])
            sent(spot(j, bx, by, c, 0, 1), s_d.at[i, j - 1])
            sent(spot(j, bx, by, c, 0, 1), s_c.at[3 + i, j - 1])
        sent(zz.at[0], s_g.at[j - 1])
    for o in range(half):
        sent(got.at[o], s_p.at[o])
    for o in range(1, half):
        sent(held.at[o - 1], s_o.at[o - 1])


def body(nd, n, states, hist_len, norm_gain, qkv_weight, output_weight, cotangent):
    dim, _, heads, size = qkv_weight.shape
    count, s, _ = states.shape
    width = heads * size
    total = count * s
    rows = NB * s
    nblk = count // NB
    half = nd // 2
    piece = dim // nd
    wqkv = qkv_weight.transpose(1, 2, 3, 0).reshape(3 * width, dim)
    wout = output_weight.reshape(width, dim)
    anywhere = pl.BlockSpec(memory_space=pl.ANY)
    dma = pltpu.SemaphoreType.DMA
    att, gst, gq, go, gg = pl.pallas_call(
        functools.partial(kernel, n, nd, s),
        out_shape=(
            jax.ShapeDtypeStruct((total, dim), BF),
            jax.ShapeDtypeStruct((total, dim), BF),
            jax.ShapeDtypeStruct((3 * width, piece), F32),
            jax.ShapeDtypeStruct((width, piece), F32),
            jax.ShapeDtypeStruct((1, piece), F32),
        ),
        in_specs=[
            pl.BlockSpec(memory_space=pltpu.SMEM),
            anywhere,
            anywhere,
            pl.BlockSpec(memory_space=pltpu.VMEM),
            anywhere,
            anywhere,
        ],
        out_specs=(anywhere,) * 5,
        scratch_shapes=[
            pltpu.VMEM((4 * dim, dim), BF),
            pltpu.VMEM((total, dim), BF),
            pltpu.VMEM((total, dim), BF),
            pltpu.VMEM((total, dim), BF),
            pltpu.VMEM((total, 1), F32),
            pltpu.VMEM((4, rows, WIN), BF),
            pltpu.VMEM((2, NB, WIN, WIN), BF),
            pltpu.VMEM((2, NB, WIN, WIN), BF),
            pltpu.VMEM((NB, s, WIN), F32),
            pltpu.VMEM((NB, s, WIN), F32),
            pltpu.VMEM((NB, s, WIN), BF),
            pltpu.VMEM((NB, s, WIN), BF),
            pltpu.VMEM((total, dim), BF),
            pltpu.VMEM((total, 3 * dim), BF),
            pltpu.VMEM((2, half, piece, 4 * WIN), BF),
            pltpu.VMEM((half, piece, 4 * WIN), BF),
            pltpu.VMEM((half - 1, piece, 4 * WIN), BF),
            pltpu.VMEM((half - 1, piece, 4 * WIN), BF),
            pltpu.VMEM((128, 4 * WIN), F32),
            pltpu.VMEM((n, 8, 128), F32),
            pltpu.VMEM((2, 2, rows, dim), BF),
            pltpu.VMEM((3 * width, piece), F32),
            pltpu.VMEM((width, piece), F32),
            pltpu.VMEM((1, piece), F32),
            dma((4,)),
            dma((2, nblk)),
            dma((2, 2)),
            dma((3,)),
            dma((n - 1,)),
            dma((n - 1,)),
            dma((2, n - 1)),
            dma((2, n - 1)),
            dma((2, n - 1)),
            dma((2, n - 1)),
            dma((5, n - 1)),
            dma((5, n - 1)),
            dma((half,)),
            dma((half,)),
            dma((half - 1,)),
            dma((half - 1,)),
            dma((n - 1,)),
            dma((n - 1,)),
        ],
        compiler_params=pltpu.CompilerParams(
            collective_id=1, has_side_effects=True, vmem_limit_bytes=60 * 1024 * 1024
        ),
        name="layer",
    )(
        hist_len,
        states.reshape(total, dim),
        cotangent.reshape(total, dim),
        norm_gain.reshape(1, dim),
        wqkv,
        wout,
    )
    return (
        att.reshape(states.shape),
        gst.reshape(states.shape),
        gq.reshape(3, heads, size, piece).transpose(3, 0, 1, 2),
        go.reshape(heads, size, piece),
        gg.reshape(piece),
    )


def solution(mesh):
    placed = (
        P("dp", None, None),
        P("dp"),
        P(),
        P(None, None, "mp", None),
        P("mp", None, None),
        P("dp", None, None),
    )
    return jax.shard_map(
        functools.partial(body, mesh.shape["dp"], mesh.shape["mp"]),
        mesh=mesh,
        in_specs=placed,
        out_specs=(
            P("dp", None, None),
            P("dp", None, None),
            P("dp", None, "mp", None),
            P("mp", None, "dp"),
            P("dp"),
        ),
        check_vma=False,
    )
```

time: 99.8 us -> 74.2 us (0.74)
  Pallas kernels: 91.3 us -> 65.6 us
  other arithmetic: 2.92 us -> 0 us
  local copies, waits for them, and re-layouts: 4.6 us -> 7.51 us
    pallas_call x3 -> x1, Pallas kernels: 91.3 us -> 65.6 us  [body(): pl.pallas_call(functools.partial(kernel, n, nd, s), out_shape=(jax.ShapeD...]
    unnamed x2 -> x13, local copies, waits for them, and re-layouts: 0.15 us -> 6.24 us
    concatenate x1 -> x0, other arithmetic: 2.39 us -> none  [body(): jnp.concatenate([qkv_weight.reshape(dim, 3 * width).T, output_weight.resh...]
    slice x3 -> x0, local copies, waits for them, and re-layouts: 1.26 us -> none  [the longest x1 0.89 us: body(): grad_qkv = grads[:, :3, :width].reshape(dim // nd, 3, heads, size)]
    reshape x2 -> x1, local copies, waits for them, and re-layouts: 2.44 us -> 1.27 us  [body(): norm_gain.reshape(1, dim)]
where the time goes in v1:
time: 74.2 us; the launch traced here: 73.7 us
  Pallas kernels  65.6 us (88%)
  local copies, waits for them, and re-layouts  7.51 us (10%)
    pallas_call x1, Pallas kernels, body(): pl.pallas_call(functools.partial(kernel, n, nd, s), out_shape=(jax.ShapeD...  65.6 us
    unnamed x13, local copies, waits for them, and re-layouts  6.24 us

profile of v1, /device:TPU:0, one launch (start us, length us, event | category | flops | bytes accessed | tf_op | source)
XLA Modules:
  0.0 73.7 jit_solution(14970281372068869154)
XLA Ops:
  0.6 1.3 %reshape.42.gain = f32[1,768]{1,0:T(1,128)} reshape(f32[768]{0:T(1024)} %param.8) | data formatting | bytes 6144 | tf_op jit(solution)/shard_map/reshape | solution.py:441
  1.9 65.6 %layer.1 = (bf16[1280,768]{1,0:T(8,128)(2,1)}, bf16[1280,768]{1,0:T(8,128)(2,1)}, f32[576,96]{1,0:T(8,128)}, f32[192,96]{1,0:T(8,128)}, f32[1,96]{1,0:T(1,128)}) custom-call(s32[16]{0:T(128)} %hist.1, bf16[1280,768]{1,0:T(8,128)(2,1)} %bitcast.13, bf16[1280,768]{1,0:T(8,128)(2,1)} %bitcast.14, f32[1,768]{1,0:T(1,128)} %reshape.42.gain, ...), custom_call_target="tpu_custom_call" | custom-call | tf_op jit(solution)/shard_map/layer/pallas_call | solution.py:371
  67.5 0.0 copy-start
  67.5 3.1 %copy.16 = bf16[16,80,768]{2,1,0:T(8,128)(2,1)} copy(bf16[16,80,768]{2,1,0:T(8,128)(2,1)} %bitcast.16) | data formatting | bytes 3932160
  70.6 0.0 copy-done
  70.6 0.0 copy-start.1
  70.6 0.0 copy-start.2
  70.6 0.0 copy-start.3
  70.6 1.3 %copy.17 = bf16[16,80,768]{2,1,0:T(8,128)(2,1)} copy(bf16[16,80,768]{2,1,0:T(8,128)(2,1)S(1)} %bitcast.15) | data formatting | bytes 3932160
  71.8 0.0 copy-done.1
  71.9 0.7 copy.18
  72.6 0.0 copy-done.2
  72.6 0.6 copy.19
  73.2 0.0 copy-done.3
  73.2 0.5 copy.20
Async XLA Ops:
  67.5 3.1 %copy-start = (bf16[1280,768]{1,0:T(8,128)(2,1)S(1)}, bf16[1280,768]{1,0:T(8,128)(2,1)}, u32[]{:S(2)}) copy-start(bf16[1280,768]{1,0:T(8,128)(2,1)} %get-tuple-element.11) | copy-start | bytes 5898244
  70.6 1.3 %copy-start.1 = (f32[576,96]{1,0:T(8,128)S(1)}, f32[576,96]{1,0:T(8,128)}, u32[]{:S(2)}) copy-start(f32[576,96]{1,0:T(8,128)} %get-tuple-element.12) | copy-start | bytes 663556
  70.6 2.0 %copy-start.2 = (f32[192,96]{1,0:T(8,128)S(1)}, f32[192,96]{1,0:T(8,128)}, u32[]{:S(2)}) copy-start(f32[192,96]{1,0:T(8,128)} %get-tuple-element.13) | copy-start | bytes 221188
  70.6 2.6 %copy-start.3 = (f32[1,96]{1,0:T(1,128)S(1)}, f32[1,96]{1,0:T(1,128)}, u32[]{:S(2)}) copy-start(f32[1,96]{1,0:T(1,128)} %get-tuple-element.14) | copy-start | bytes 1156

commit v2 on v1

--- a/solution.py
+++ b/solution.py
@@ -10,6 +10,32 @@
 LEVELS = 4
 NB = 4
 WIN = 256
+PLAN = (
+    ((0, 2), "a", 1, 0),
+    ((0, 3), "a", 1, 1),
+    (("g", 1), "b", 1, 0),
+    (("g", 3), "b", 1, 1),
+    (("s", 1), "c", 1, 0),
+    (("s", 1), "c", 1, 1),
+    (("s", 1), "a", 2, 0),
+    (("s", 1), "d", 1),
+    ((1, 0), "a", 2, 1),
+    ((1, 2), "b", 2, 0),
+    ((1, 3), "b", 2, 1),
+    ((1, 3), "a", 3, 0),
+    ((1, 3), "a", 3, 1),
+    (("s", 2), "c", 2, 0),
+    (("s", 2), "c", 2, 1),
+    (("s", 2), "d", 2),
+    ((2, 1), "b", 3, 0),
+    ((2, 2), "b", 3, 1),
+    ((2, 3), "c", 3, 0),
+    ((2, 3), "chip"),
+    (("s", 3), "c", 3, 1),
+    (("s", 3), "d", 3),
+    ((4, 1), "sum"),
+    (("s", 5), "gain"),
+)
 BF = jnp.bfloat16
 F32 = jnp.float32
 MESH = pl.DeviceIdType.MESH
@@ -35,8 +61,25 @@
     partner = (d + 1 - 2 * c, z)
     across = ((d + 2 - 4 * bx, z), (d + 4 - 8 * by, z))
     others = [(((chip + o) % half) * 2 + c, z) for o in range(1, half)]
-    zpeers = [(d, (z + n - j) % n) for j in range(1, n)]
-
+    near = [sorted((abs(k - m), -abs(2 * k + 1 - n), k) for k in range(n) if k != m) for m in range(n)]
+    near = [[one[-1] for one in row] for row in near]
+    away = [row[:1] + row[:0:-1] if m in (0, n - 1) else row for m, row in enumerate(near)]
+
+    def lookup(table):
+        value = table[0]
+        for k in range(1, n):
+            value = jnp.where(z == k, table[k], value)
+        return value
+
+    peer = [None] + [lookup([near[k][m] for k in range(n)]) for m in range(n - 1)]
+    goal = [None] + [lookup([away[k][m] for k in range(n)]) for m in range(n - 1)]
+    seat = [None] + [lookup([near[away[k][m]].index(k) + 1 for k in range(n)]) for m in range(n - 1)]
+    zpeers = [None] + [(d, goal[j]) for j in range(1, n)]
+
+    barrier = pltpu.get_barrier_semaphore()
+    greet = zpeers[1:] + others + [partner]
+    for device in greet:
+        pl.semaphore_signal(barrier, inc=1, device_id=device, device_id_type=MESH)
     loads = []
     for k in range(3):
         loads.append(pltpu.make_async_copy(
@@ -49,16 +92,11 @@
         pltpu.make_async_copy(states.at[at], st.at[at], s_in.at[0, i]).start()
         pltpu.make_async_copy(cot.at[at], mc.at[at], s_in.at[1, i]).start()
 
-    barrier = pltpu.get_barrier_semaphore()
-    greet = zpeers + others + [partner]
-    for device in greet:
-        pl.semaphore_signal(barrier, inc=1, device_id=device, device_id_type=MESH)
     pj[...] = jnp.zeros_like(pj)
     sq[...] = jnp.zeros_like(sq)
     sg[...] = jnp.zeros_like(sg)
     for copy in loads:
         copy.wait()
-    pl.semaphore_wait(barrier, len(greet))
 
     def remote(src, dst, ssem, rsem, device):
         return pltpu.make_async_remote_copy(
@@ -70,47 +108,44 @@
 
     quarter = width // 4
 
-    def spot(j, x, y, core, i=0, count=2):
-        first = pl.multiple_of((x + 2 * y) * dim + place[j] * width + (2 * core + i) * quarter, 16)
-        return wall.at[pl.ds(first, count * quarter)]
-
-    order = [j for j in (1, n - 1) if j < n] + [j for j in range(2, n - 1)]
-    place = {j: m for m, j in enumerate([0] + order)}
+    def spot(j, x, y, core, i):
+        first = pl.multiple_of((x + 2 * y) * dim + j * width + (2 * core + i) * quarter, 16)
+        return wall.at[pl.ds(first, quarter)]
+
 
     def send_own():
-        mine = spot(0, bx, by, c)
-        for j in order:
-            remote(mine, spot(j, bx, by, c), s_z.at[j - 1], r_z.at[j - 1], zpeers[j - 1]).start()
-
-    def first_hop(j):
-        here = spot(j, bx, by, c)
-        arrived(here, r_z.at[j - 1])
+        for j in range(1, n):
+            for e in range(2):
+                remote(spot(0, bx, by, c, e), spot(seat[j], bx, by, c, e),
+                       s_z.at[j - 1, e], r_z.at[seat[j] - 1, e], zpeers[j]).start()
+
+    def first_hop(j, e):
+        here = spot(j, bx, by, c, e)
+        arrived(here, r_z.at[j - 1, e])
         for i in range(2):
-            remote(here, here, s_x.at[i, j - 1], r_x.at[i, j - 1], across[i]).start()
-        remote(here, here, s_c.at[0, j - 1], r_c.at[0, j - 1], partner).start()
+            remote(here, here, s_x.at[i, j - 1, e], r_x.at[i, j - 1, e], across[i]).start()
+        remote(here, here, s_c.at[0, j - 1, e], r_c.at[0, j - 1, e], partner).start()
 
     sides = ((1 - bx, by), (bx, 1 - by))
     diag = (1 - bx, 1 - by)
 
-    def second_hop(j):
-        for i in range(2):
-            here = spot(j, *sides[i], c)
-            arrived(here, r_x.at[i, j - 1])
-            one = spot(j, *sides[i], c, i, 1)
-            remote(one, one, s_d.at[i, j - 1], r_d.at[i, j - 1], across[1 - i]).start()
-            remote(here, here, s_c.at[1 + i, j - 1], r_c.at[1 + i, j - 1], partner).start()
-
-    def third_hop(j):
-        for i in range(2):
-            one = spot(j, *diag, c, i, 1)
-            arrived(one, r_d.at[i, j - 1])
-            remote(one, one, s_c.at[3 + i, j - 1], r_c.at[3 + i, j - 1], partner).start()
+    def second_hop(j, e):
+        for i in (e, 1 - e):
+            here = spot(j, *sides[i], c, e)
+            arrived(here, r_x.at[i, j - 1, e])
+            if i == e:
+                remote(here, here, s_d.at[j - 1, e], r_d.at[j - 1, e], across[1 - i]).start()
+            remote(here, here, s_c.at[1 + i, j - 1, e], r_c.at[1 + i, j - 1, e], partner).start()
+
+    def third_hop(j, e):
+        here = spot(j, *diag, c, e)
+        arrived(here, r_d.at[j - 1, e])
+        remote(here, here, s_c.at[3, j - 1, e], r_c.at[3, j - 1, e], partner).start()
 
     def landed(j):
-        for k, (x, y) in enumerate(((bx, by),) + sides):
-            arrived(spot(j, x, y, 1 - c), r_c.at[k, j - 1])
-        for i in range(2):
-            arrived(spot(j, *diag, 1 - c, i, 1), r_c.at[3 + i, j - 1])
+        for e in range(2):
+            for k, (x, y) in enumerate(((bx, by),) + sides + (diag,)):
+                arrived(spot(j, x, y, 1 - c, e), r_c.at[k, j - 1, e])
 
     scatter_order = list(range(1, half)) + [0]
 
@@ -139,26 +174,29 @@
         pick = (row - piece * d == column).astype(F32).astype(BF)
         gsum = jnp.zeros((1, 128), F32)
         for k in range(4):
-            turned = tot[:, k * WIN : (k + 1) * WIN].T[:width]
+            m = 4 + k // 2
+            turned = jnp.concatenate(
+                [tot[:, k * 128 : (k + 1) * 128].T, tot[:, m * 128 : (m + 1) * 128].T[64 * (k % 2) : 64 * (k % 2) + 64]], axis=0
+            )
             if k < 3:
                 gqv[k * width : (k + 1) * width, :] = turned[:, :piece]
                 mine = dot(wall[k * dim : k * dim + width, :], pick, 1, 0)
                 gsum = gsum + jnp.sum(mine * turned, axis=0, keepdims=True)
             else:
                 gov[...] = turned[:, :piece]
-        scale = gain[...]
+        scale = gain[...].reshape(1, dim)
         own_gain = jnp.ones((1, piece), F32)
         for t in range(nd):
             own_gain = jnp.where(d == t, scale[:, t * piece : (t + 1) * piece], own_gain)
         zz[z, 0:1, :piece] = gsum[:, :piece] / own_gain
         for j in range(1, n):
-            remote(zz.at[z], zz.at[z], s_g.at[j - 1], r_g.at[j - 1], zpeers[j - 1]).start()
+            remote(zz.at[z], zz.at[z], s_g.at[j - 1], r_g.at[seat[j] - 1], zpeers[j]).start()
         pltpu.make_async_copy(gqv, gq, s_res.at[0]).start()
         pltpu.make_async_copy(gov, go, s_res.at[1]).start()
 
     def gain_sum():
         for j in range(1, n):
-            arrived(zz.at[(z + j) % n], r_g.at[j - 1])
+            arrived(zz.at[peer[j]], r_g.at[j - 1])
         value = zz[0, 0:1, :piece]
         for k in range(1, n):
             value = value + zz[k, 0:1, :piece]
@@ -200,13 +238,21 @@
             ref[at, base : base + 256] = x
 
     def prepare(i):
+        def fresh():
+            at = pl.ds(pl.multiple_of(i * rows, 16), rows)
+            pltpu.make_async_copy(states.at[at], st.at[at], s_in.at[0, i]).wait()
+            pltpu.make_async_copy(cot.at[at], mc.at[at], s_in.at[1, i]).wait()
+
+        if isinstance(i, int):
+            fresh()
+        else:
+            pl.when(i < nblk)(fresh)
+            i = i % nblk
         at = pl.ds(pl.multiple_of(i * rows, 16), rows)
-        pltpu.make_async_copy(states.at[at], st.at[at], s_in.at[0, i]).wait()
-        pltpu.make_async_copy(cot.at[at], mc.at[at], s_in.at[1, i]).wait()
         wide = st[at, :].astype(F32)
         scale = lax.rsqrt(jnp.mean(wide * wide, axis=-1, keepdims=True) + 1e-06)
         inv[at, :] = scale
-        normed[at, :] = (wide * scale * gain[...]).astype(BF)
+        normed[at, :] = (wide * scale * gain[...].reshape(1, dim)).astype(BF)
         pos = lax.broadcasted_iota(jnp.int32, (s, dim), 0)
         for b in range(NB):
             one = pl.ds(pl.multiple_of(i * rows + b * s, 16), s)
@@ -257,13 +303,22 @@
                 scores(b + 2)
             outs(b)
 
-    def weight_grads():
+    def weight_grads(run):
+        kept = None
         for k in range(4):
+            run(("g", k))
             lhs = normed[...] if k < 3 else mc[...]
             rhs = gproj[:, k * dim : k * dim + WIN] if k < 3 else ctx[:, :WIN]
             acc = dot(lhs, rhs, 0, 0)
+            if k % 2:
+                both = kept + pltpu.roll(acc[:, 128:], 64, 1)
             for t in range(nd):
-                part[t % 2, t // 2, :, k * WIN : (k + 1) * WIN] = acc[t * piece : (t + 1) * piece].astype(BF)
+                here = slice(t * piece, (t + 1) * piece)
+                part[t % 2, t // 2, :, k * 128 : (k + 1) * 128] = acc[here, :128].astype(BF)
+                if k % 2:
+                    m = 4 + k // 2
+                    part[t % 2, t // 2, :, m * 128 : (m + 1) * 128] = both[here].astype(BF)
+            kept = acc[:, 128:]
 
     def results(i):
         at = pl.ds(pl.multiple_of(i * rows, 16), rows)
@@ -281,7 +336,7 @@
         gn = dot(gproj[at, :], wall[: 3 * dim, :], 1, 0)
         scale = inv[at, :]
         unit = wide * scale
-        gu = gn * gain[...]
+        gu = gn * gain[...].reshape(1, dim)
         corr = jnp.mean(gu * unit, axis=-1, keepdims=True)
         res[1, i % 2] = (mc[at, :].astype(F32) + scale * (gu - unit * corr)).astype(BF)
         for copy in copies:
@@ -295,38 +350,47 @@
                     for one in step:
                         one()
 
-    plan = {stage: [[] for _ in range(nblk)] for stage in range(n)}
-
-    def note(stage, i, step, *args):
-        spots = [(a, b) for a in range(n) for b in range(nblk)]
-        place = min(stage * nblk + i, len(spots) - 1)
-        a, b = spots[place]
-        plan[a][b].append(functools.partial(step, *args))
-
-    tail = []
-    for m, j in enumerate(order):
-        begin = m * nblk
-        note(0, begin + 1, first_hop, j)
-        note(0, begin + 2, second_hop, j)
-        note(0, begin + 3, third_hop, j)
-        plan[m + 1][0].insert(0, functools.partial(landed, j))
-    note(1, 1, scatter_chip)
-    note(2, 1, scatter_sum)
-    note(3, 1, gain_sum)
-
+    plan = {}
+
+    def note(when, step, *args):
+        plan.setdefault(when, []).append(functools.partial(step, *args))
+
+    for when, step, *args in PLAN:
+        note(when, {"a": first_hop, "b": second_hop, "c": third_hop, "d": landed, "chip": scatter_chip,
+                    "sum": scatter_sum, "gain": gain_sum}[step], *args)
+
+    def steps(kind):
+        return [plan.get((kind, i), ()) for i in range(nblk)]
+
+    def run(when):
+        for one in plan.get(when, ()):
+            one()
+
+    prepare(0)
+    pl.semaphore_wait(barrier, len(greet))
     send_own()
     for m in range(n):
+        run(("s", m))
+
         @pl.loop(0, nblk)
         def _(i):
-            at_step(i, plan[m])
+            at_step(i, steps(m))
             if m == 0:
-                prepare(i)
+                prepare(i + 1)
             attention(m, i)
+
         if m == 0:
-            weight_grads()
+            weight_grads(run)
             scatter_core()
 
-    pl.loop(0, nblk)(results)
+    run(("s", n))
+
+    @pl.loop(0, nblk)
+    def _(i):
+        at_step(i, steps(n))
+        results(i)
+
+    run(("s", n + 1))
 
     for i in range(max(nblk - 2, 0), nblk):
         at = pl.ds(i * rows, rows)
@@ -339,20 +403,58 @@
     def sent(src, ssem):
         remote(src, src, ssem, ssem, partner).wait_send()
 
-    for j in order:
-        here = spot(j, bx, by, c)
-        sent(here, s_z.at[j - 1])
-        sent(here, s_c.at[0, j - 1])
-        for i in range(2):
-            sent(here, s_x.at[i, j - 1])
-            sent(here, s_c.at[1 + i, j - 1])
-            sent(spot(j, bx, by, c, 0, 1), s_d.at[i, j - 1])
-            sent(spot(j, bx, by, c, 0, 1), s_c.at[3 + i, j - 1])
+    for j in range(1, n):
+        for e in range(2):
+            here = spot(j, bx, by, c, e)
+            for sem in [s_z.at[j - 1, e], s_d.at[j - 1, e]]:
+                sent(here, sem)
+            for i in range(2):
+                sent(here, s_x.at[i, j - 1, e])
+            for k in range(4):
+                sent(here, s_c.at[k, j - 1, e])
         sent(zz.at[0], s_g.at[j - 1])
     for o in range(half):
         sent(got.at[o], s_p.at[o])
     for o in range(1, half):
         sent(held.at[o - 1], s_o.at[o - 1])
+
+
+def settle_kernel(count, *refs):
+    srcs, dsts, (big, *small), (sem_in, sem_out) = refs[:5], refs[5:10], refs[10:14], refs[14:]
+    rows = big.shape[2]
+    ins, outs = [], []
+    for i in range(count):
+        for k in range(2):
+            at = pl.ds(i * rows, rows)
+            ins.append(pltpu.make_async_copy(srcs[k].at[at], big.at[k, i], sem_in.at[len(ins)]))
+            outs.append(pltpu.make_async_copy(big.at[k, i], dsts[k].at[at], sem_out.at[len(outs)]))
+    for k in range(3):
+        ins.append(pltpu.make_async_copy(srcs[2 + k], small[k], sem_in.at[len(ins)]))
+        outs.append(pltpu.make_async_copy(small[k], dsts[2 + k], sem_out.at[len(outs)]))
+    for copy in ins:
+        copy.start()
+    for one, other in zip(ins, outs):
+        one.wait()
+        other.start()
+    for copy in outs:
+        copy.wait()
+
+
+def settle(arrays):
+    count = 4
+    rows, dim = arrays[0].shape
+    anywhere = pl.BlockSpec(memory_space=pl.ANY)
+    return pl.pallas_call(
+        functools.partial(settle_kernel, count),
+        out_shape=tuple(jax.ShapeDtypeStruct(a.shape, a.dtype) for a in arrays),
+        in_specs=(anywhere,) * 5,
+        out_specs=(anywhere,) * 5,
+        scratch_shapes=[pltpu.VMEM((2, count, rows // count, dim), BF)]
+        + [pltpu.VMEM(a.shape, a.dtype) for a in arrays[2:]]
+        + [pltpu.SemaphoreType.DMA((2 * count + 3,))] * 2,
+        compiler_params=pltpu.CompilerParams(vmem_limit_bytes=60 * 1024 * 1024),
+        name="settle",
+    )(*arrays)
 
 
 def body(nd, n, states, hist_len, norm_gain, qkv_weight, output_weight, cotangent):
@@ -401,11 +503,11 @@
             pltpu.VMEM((NB, s, WIN), BF),
             pltpu.VMEM((total, dim), BF),
             pltpu.VMEM((total, 3 * dim), BF),
-            pltpu.VMEM((2, half, piece, 4 * WIN), BF),
-            pltpu.VMEM((half, piece, 4 * WIN), BF),
-            pltpu.VMEM((half - 1, piece, 4 * WIN), BF),
-            pltpu.VMEM((half - 1, piece, 4 * WIN), BF),
-            pltpu.VMEM((128, 4 * WIN), F32),
+            pltpu.VMEM((2, half, piece, dim), BF),
+            pltpu.VMEM((half, piece, dim), BF),
+            pltpu.VMEM((half - 1, piece, dim), BF),
+            pltpu.VMEM((half - 1, piece, dim), BF),
+            pltpu.VMEM((128, dim), F32),
             pltpu.VMEM((n, 8, 128), F32),
             pltpu.VMEM((2, 2, rows, dim), BF),
             pltpu.VMEM((3 * width, piece), F32),
@@ -415,14 +517,14 @@
             dma((2, nblk)),
             dma((2, 2)),
             dma((3,)),
-            dma((n - 1,)),
-            dma((n - 1,)),
-            dma((2, n - 1)),
-            dma((2, n - 1)),
-            dma((2, n - 1)),
-            dma((2, n - 1)),
-            dma((5, n - 1)),
-            dma((5, n - 1)),
+            dma((n - 1, 2)),
+            dma((n - 1, 2)),
+            dma((2, n - 1, 2)),
+            dma((2, n - 1, 2)),
+            dma((n - 1, 2)),
+            dma((n - 1, 2)),
+            dma((4, n - 1, 2)),
+            dma((4, n - 1, 2)),
             dma((half,)),
             dma((half,)),
             dma((half - 1,)),
@@ -438,10 +540,11 @@
         hist_len,
         states.reshape(total, dim),
         cotangent.reshape(total, dim),
-        norm_gain.reshape(1, dim),
+        norm_gain,
         wqkv,
         wout,
     )
+    att, gst, gq, go, gg = settle((att, gst, gq, go, gg))
     return (
         att.reshape(states.shape),
         gst.reshape(states.shape),

time: 74.2 us -> 59.2 us (0.80)
  local copies, waits for them, and re-layouts: 7.51 us -> 0 us
  Pallas kernels: 65.6 us -> 58.4 us
    pallas_call x1, Pallas kernels: 65.6 us -> 54.7 us  [body(): pl.pallas_call(functools.partial(kernel, n, nd, s), out_shape=(jax.ShapeD...]
    unnamed x13 -> x0, local copies, waits for them, and re-layouts: 6.24 us -> none
    pallas_call x0 -> x1, Pallas kernels: none -> 3.64 us  [settle(): pl.pallas_call(functools.partial(settle_kernel, count), out_shape=tuple((...]
    reshape x1 -> x0, local copies, waits for them, and re-layouts: 1.27 us -> none  [body(): norm_gain.reshape(1, dim)]
where the time goes in v2:
time: 59.2 us; the launch traced here: 59 us
  Pallas kernels  58.4 us (99%)
  between operations  0.64 us (1%)
    pallas_call x1, Pallas kernels, body(): pl.pallas_call(functools.partial(kernel, n, nd, s), out_shape=(jax.ShapeD...  54.7 us
    pallas_call x1, Pallas kernels, settle(): pl.pallas_call(functools.partial(settle_kernel, count), out_shape=tuple((...  3.64 us

profile of v2, /device:TPU:0, one launch (start us, length us, event | category | flops | bytes accessed | tf_op | source)
XLA Modules:
  0.0 59.0 jit_solution(357905395476966452)
XLA Ops:
  0.6 54.7 %layer.1 = (bf16[1280,768]{1,0:T(8,128)(2,1)}, bf16[1280,768]{1,0:T(8,128)(2,1)}, f32[576,96]{1,0:T(8,128)}, f32[192,96]{1,0:T(8,128)}, f32[1,96]{1,0:T(1,128)}) custom-call(s32[16]{0:T(128)} %hist.1, bf16[1280,768]{1,0:T(8,128)(2,1)} %bitcast.13, bf16[1280,768]{1,0:T(8,128)(2,1)} %bitcast.14, f32[768]{0:T(1024)} %gain.1, bf16[576,768]{1,0:T(8,128)(2,1)} %bitcast.15, ...), custom_call_target="tpu_custom_call" | custom-call | tf_op jit(solution)/shard_map/layer/pallas_call | solution.py:473
  55.4 3.6 %settle.1 = (bf16[1280,768]{1,0:T(8,128)(2,1)}, bf16[1280,768]{1,0:T(8,128)(2,1)}, f32[576,96]{1,0:T(8,128)}, f32[192,96]{1,0:T(8,128)}, f32[1,96]{1,0:T(1,128)}) custom-call(bf16[1280,768]{1,0:T(8,128)(2,1)} %get-tuple-element.15.refs_0_, bf16[1280,768]{1,0:T(8,128)(2,1)} %get-tuple-element.16.refs_1_, f32[576,96]{1,0:T(8,128)} %get-tuple-element.17.refs_2_, ...), custom_call_target="tpu_custom_call" | custom-call | tf_op jit(solution)/shard_map/settle/pallas_call | solution.py:447

commit v3 on v2

--- a/solution.py
+++ b/solution.py
@@ -8,32 +8,43 @@
 from jax.sharding import PartitionSpec as P
 
 LEVELS = 4
-NB = 4
+NB = 8
 WIN = 256
+CHUNK = 32
 PLAN = (
-    ((0, 2), "a", 1, 0),
-    ((0, 3), "a", 1, 1),
-    (("g", 1), "b", 1, 0),
-    (("g", 3), "b", 1, 1),
+    ((0, 1), "z", 1, 0),
+    ((0, 1), "a", 1, 0),
+    ((0, 1), "in-z", 2, 0),
+    (((0, "mid"), 1), "z", 1, 1),
+    (((0, "mid"), 1), "a", 1, 1),
+    (((0, "mid"), 1), "in-z", 2, 1),
+    (("g", 2), "b", 1, 0),
+    (("g", 2), "out-z", 2, 0),
+    (("g", 2), "in-z", 3, 0),
+    (("s", 1), "b", 1, 1),
+    (("g", 2), "a", 2, 0),
+    (("s", 1), "out-z", 2, 1),
+    (("s", 1), "in-z", 3, 1),
+    (("s", 1), "a", 2, 1),
     (("s", 1), "c", 1, 0),
     (("s", 1), "c", 1, 1),
-    (("s", 1), "a", 2, 0),
     (("s", 1), "d", 1),
-    ((1, 0), "a", 2, 1),
-    ((1, 2), "b", 2, 0),
-    ((1, 3), "b", 2, 1),
-    ((1, 3), "a", 3, 0),
-    ((1, 3), "a", 3, 1),
-    (("s", 2), "c", 2, 0),
+    ((1, 0), "b", 2, 0),
+    (((1, "mid"), 0), "out-z", 3, 0),
+    (((1, "mid"), 0), "b", 2, 1),
+    (((1, "mid"), 0), "a", 3, 0),
+    ((1, 1), "out-z", 3, 1),
+    ((1, 1), "a", 3, 1),
+    (((1, "mid"), 1), "c", 2, 0),
     (("s", 2), "c", 2, 1),
     (("s", 2), "d", 2),
-    ((2, 1), "b", 3, 0),
-    ((2, 2), "b", 3, 1),
-    ((2, 3), "c", 3, 0),
-    ((2, 3), "chip"),
-    (("s", 3), "c", 3, 1),
+    (((2, "mid"), 0), "b", 3, 0),
+    ((2, 1), "b", 3, 1),
+    (("p", 1), "chip"),
+    (("p", 0), "c", 3, 0),
+    (("p", 1), "c", 3, 1),
     (("s", 3), "d", 3),
-    ((4, 1), "sum"),
+    (("f", 1), "sum"),
     (("s", 5), "gain"),
 )
 BF = jnp.bfloat16
@@ -46,9 +57,9 @@
 
 
 def kernel(n, nd, s, hist, states, cot, gain, wqkv, wout, att, gst, gq, go, gg,
-           wall, st, mc, normed, inv, pj, sq, sg, scb, gpb, pbb, dsb, ctx, gproj,
+           wall, st, mc, normed, inv, pj, sq, sg, scb, gpb, pbb, dsb, ctx, gproj, ga, aa,
            part, got, total, held, tot, zz, res, gqv, gov, ggv,
-           s_w, s_in, s_out, s_res, s_z, r_z, s_x, r_x, s_d, r_d, s_c, r_c, s_p, r_p, s_o, r_o, s_g, r_g):
+           s_w, s_in, s_out, s_res, s_z, s_r, r_z, s_x, r_x, s_d, r_d, s_c, r_c, s_p, r_p, s_o, r_o, s_g, r_g):
     rows_all, dim = st.shape
     width = wout.shape[0]
     rows = NB * s
@@ -113,15 +124,39 @@
         return wall.at[pl.ds(first, quarter)]
 
 
+    inner = jnp.logical_and(z > 0, z < n - 1)
+    steps_z = (-1, 1)
+    fits = [z > 0, z < n - 1]
+    next_z = [(d, (z + n - 1) % n), (d, (z + 1) % n)]
+
+    def seat_at(m, source):
+        return near[m].index(source) + 1 if 0 <= m < n else 1
+
+    own_seat = [lookup([seat_at(k + step, k) for k in range(n)]) for step in steps_z]
+    onward = [None] + [[lookup([int(near[k][m] * step < k * step and 0 <= k + step < n) for k in range(n)])
+                        for step in steps_z] for m in range(n - 1)]
+    pass_seat = [None] + [[lookup([seat_at(k + step, near[k][m]) if near[k][m] * step < k * step else 1 for k in range(n)])
+                           for step in steps_z] for m in range(n - 1)]
+
     def send_own():
-        for j in range(1, n):
-            for e in range(2):
-                remote(spot(0, bx, by, c, e), spot(seat[j], bx, by, c, e),
-                       s_z.at[j - 1, e], r_z.at[seat[j] - 1, e], zpeers[j]).start()
+        for way in range(2):
+            @pl.when(fits[way])
+            def _():
+                for e in range(2):
+                    remote(spot(0, bx, by, c, e), spot(own_seat[way], bx, by, c, e),
+                           s_z.at[way, e], r_z.at[own_seat[way] - 1, e], next_z[way]).start()
+
+    def relay(j, e):
+        here = spot(j, bx, by, c, e)
+        arrived(here, r_z.at[j - 1, e])
+        for way in range(2):
+            @pl.when(onward[j][way] == 1)
+            def _():
+                remote(here, spot(pass_seat[j][way], bx, by, c, e),
+                       s_r.at[j - 1, e], r_z.at[pass_seat[j][way] - 1, e], next_z[way]).start()
 
     def first_hop(j, e):
         here = spot(j, bx, by, c, e)
-        arrived(here, r_z.at[j - 1, e])
         for i in range(2):
             remote(here, here, s_x.at[i, j - 1, e], r_x.at[i, j - 1, e], across[i]).start()
         remote(here, here, s_c.at[0, j - 1, e], r_c.at[0, j - 1, e], partner).start()
@@ -248,16 +283,19 @@
         else:
             pl.when(i < nblk)(fresh)
             i = i % nblk
-        at = pl.ds(pl.multiple_of(i * rows, 16), rows)
-        wide = st[at, :].astype(F32)
-        scale = lax.rsqrt(jnp.mean(wide * wide, axis=-1, keepdims=True) + 1e-06)
-        inv[at, :] = scale
-        normed[at, :] = (wide * scale * gain[...].reshape(1, dim)).astype(BF)
-        pos = lax.broadcasted_iota(jnp.int32, (s, dim), 0)
+        scaled_gain = gain[...].reshape(1, dim)
+        for first in range(0, rows, CHUNK):
+            some = pl.ds(pl.multiple_of(i * rows + first, 16), CHUNK)
+            wide = st[some, :].astype(F32)
+            scale = lax.rsqrt(jnp.mean(wide * wide, axis=-1, keepdims=True) + 1e-06)
+            inv[some, :] = scale
+            normed[some, :] = (wide * scale * scaled_gain).astype(BF)
+        pos = lax.broadcasted_iota(jnp.int32, (16, 1), 0)
         for b in range(NB):
-            one = pl.ds(pl.multiple_of(i * rows + b * s, 16), s)
-            keep = pos < LEVELS * hist[i * NB + b]
-            mc[one, :] = jnp.where(keep, mc[one, :].astype(F32), 0.0).astype(BF)
+            for first in range(0, s, 16):
+                some = pl.ds(pl.multiple_of(i * rows + b * s + first, 16), 16)
+                keep = (pos + first < LEVELS * hist[i * NB + b]).astype(F32)
+                mc[some, :] = jnp.where(keep > 0.0, mc[some, :].astype(F32), 0.0).astype(BF)
 
     def attention(slot, i):
         odd = slot % 2
@@ -265,48 +303,70 @@
         first = slot * width - 64 * odd
         cols = width + 64 * odd
         at = pl.ds(pl.multiple_of(i * rows, 16), rows)
-        for k in range(4):
+
+        def project(k):
             lhs = normed[at, :] if k < 3 else mc[at, :]
             pj[k, :, :cols] = dot(lhs, wall[k * dim + first : k * dim + first + cols, :], 1, 1).astype(BF)
 
-        def scores(b):
-            mine = slice(b * s, (b + 1) * s)
-            spread(pj[0, mine, :], sq.at[odd, b], odd)
-            spread(pj[3, mine, :], sg.at[odd, b], odd)
-            scb[b] = dot(pj[1, mine, :], sq[odd, b], 1, 1)
-            gpb[b] = dot(pj[2, mine, :], sg[odd, b], 1, 1)
+        def mine(b):
+            return slice(b * s, (b + 1) * s)
+
+        def there(b):
+            return pl.ds(pl.multiple_of(i * rows + b * s, 16), s)
+
+        def score(b):
+            spread(pj[0, mine(b), :], sq.at[odd, b], odd)
+            scb[b] = dot(pj[1, mine(b), :], sq[odd, b], 1, 1)
 
         def soft(b):
             keep = key_pos < LEVELS * hist[i * NB + b]
             sc = jnp.where(keep, scb[b], -1e30)
             ex = jnp.exp(sc - jnp.max(sc, axis=0, keepdims=True))
             prob = ex * (1.0 / jnp.sum(ex, axis=0, keepdims=True))
+            scb[b] = prob
             pbb[b] = prob.astype(BF)
-            gp = gpb[b]
+
+        def weigh(b):
+            spread(pj[3, mine(b), :], sg.at[odd, b], odd)
+            gpb[b] = dot(pj[2, mine(b), :], sg[odd, b], 1, 1)
+
+        def slope(b):
+            prob, gp = scb[b], gpb[b]
             delta = jnp.sum(prob * gp, axis=0, keepdims=True)
             dsb[b] = (prob * (gp - delta)).astype(BF)
 
-        def outs(b):
-            mine = slice(b * s, (b + 1) * s)
-            one = pl.ds(pl.multiple_of(i * rows + b * s, 16), s)
-            pb, ds = pbb[b], dsb[b]
-            put(gproj, one, dim + base, dot(ds, sq[odd, b], 1, 0), odd)
-            put(gproj, one, 2 * dim + base, dot(pb, sg[odd, b], 1, 0), odd)
-            put(ctx, one, base, fold(dot(pb, pj[2, mine, :], 0, 0), odd), odd)
-            put(gproj, one, base, fold(dot(ds, pj[1, mine, :], 0, 0), odd), odd)
-
-        scores(0)
-        scores(1)
-        for b in range(NB):
-            soft(b)
-            if b + 2 < NB:
-                scores(b + 2)
-            outs(b)
+        def value_grad(b):
+            put(gproj, there(b), 2 * dim + base, dot(pbb[b], sg[odd, b], 1, 0), odd)
+
+        def mix(b):
+            put(ctx, there(b), base, fold(dot(pbb[b], pj[2, mine(b), :], 0, 0), odd), odd)
+
+        def score_side(b):
+            ds = dsb[b]
+            put(gproj, there(b), dim + base, dot(ds, sq[odd, b], 1, 0), odd)
+            put(gproj, there(b), base, fold(dot(ds, pj[1, mine(b), :], 0, 0), odd), odd)
+
+        every = range(NB)
+        for k in range(4):
+            project(k)
+        at_step(i, steps((slot, "mid")))
+        for b in range(NB + 2):
+            if b < NB:
+                score(b)
+                weigh(b)
+            if b >= 2:
+                value_grad(b - 2)
+                mix(b - 2)
+                score_side(b - 2)
+            if 1 <= b <= NB:
+                soft(b - 1)
+                slope(b - 1)
 
     def weight_grads(run):
         kept = None
         for k in range(4):
-            run(("g", k))
+            if k % 2 == 0:
+                run(("g", k))
             lhs = normed[...] if k < 3 else mc[...]
             rhs = gproj[:, k * dim : k * dim + WIN] if k < 3 else ctx[:, :WIN]
             acc = dot(lhs, rhs, 0, 0)
@@ -320,27 +380,50 @@
                     part[t % 2, t // 2, :, m * 128 : (m + 1) * 128] = both[here].astype(BF)
             kept = acc[:, 128:]
 
-    def results(i):
+    early = dim - WIN
+
+    def gather_terms(at, low, high):
+        gn = None
+        for k in range(3):
+            term = dot(gproj[at, k * dim + low : k * dim + high], wall[k * dim + low : k * dim + high, :], 1, 0)
+            gn = term if gn is None else gn + term
+        return gn, dot(ctx[at, low:high], wall[3 * dim + low : 3 * dim + high, :], 1, 0)
+
+    def partial(i):
         at = pl.ds(pl.multiple_of(i * rows, 16), rows)
-        wide = st[at, :].astype(F32)
+        ga[at, :], aa[at, :] = gather_terms(at, 0, early)
+
+    def rest(i):
+        at = pl.ds(pl.multiple_of(i * rows, 16), rows)
+        gn, mixed = gather_terms(at, early, dim)
+        ga[at, :] += gn
+        aa[at, :] += mixed
+
+    def finish(i):
+        at = pl.ds(pl.multiple_of(i * rows, 16), rows)
         copies = [
             pltpu.make_async_copy(res.at[k, i % 2], (att, gst)[k].at[at], s_out.at[k, i % 2]) for k in range(2)
         ]
-
-        @pl.when(i >= 2)
-        def _():
-            for copy in copies:
+        if isinstance(i, int):
+            for copy in copies if i >= 2 else ():
                 copy.wait()
-
-        res[0, i % 2] = (wide + dot(ctx[at, :], wall[3 * dim :, :], 1, 0)).astype(BF)
-        gn = dot(gproj[at, :], wall[: 3 * dim, :], 1, 0)
-        scale = inv[at, :]
-        unit = wide * scale
-        gu = gn * gain[...].reshape(1, dim)
-        corr = jnp.mean(gu * unit, axis=-1, keepdims=True)
-        res[1, i % 2] = (mc[at, :].astype(F32) + scale * (gu - unit * corr)).astype(BF)
-        for copy in copies:
-            copy.start()
+        else:
+            @pl.when(i >= 2)
+            def _():
+                for copy in copies:
+                    copy.wait()
+
+        scaled_gain = gain[...].reshape(1, dim)
+        for first in range(0, rows, CHUNK):
+            some = pl.ds(pl.multiple_of(i * rows + first, 16), CHUNK)
+            wide = st[some, :].astype(F32)
+            res[0, i % 2, first : first + CHUNK] = (wide + aa[some, :]).astype(BF)
+            scale = inv[some, :]
+            unit = wide * scale
+            gu = ga[some, :] * scaled_gain
+            corr = jnp.mean(gu * unit, axis=-1, keepdims=True)
+            res[1, i % 2, first : first + CHUNK] = (mc[some, :].astype(F32) + scale * (gu - unit * corr)).astype(BF)
+        return copies
 
     def at_step(i, steps):
         for k, step in enumerate(steps):
@@ -355,9 +438,16 @@
     def note(when, step, *args):
         plan.setdefault(when, []).append(functools.partial(step, *args))
 
+    def only(side, step):
+        def run_it(*args):
+            pl.when(inner if side == "in" else jnp.logical_not(inner))(functools.partial(step, *args))
+        return run_it
+
     for when, step, *args in PLAN:
-        note(when, {"a": first_hop, "b": second_hop, "c": third_hop, "d": landed, "chip": scatter_chip,
-                    "sum": scatter_sum, "gain": gain_sum}[step], *args)
+        where, _, step = step.rpartition("-")
+        action = {"z": relay, "a": first_hop, "b": second_hop, "c": third_hop, "d": landed, "chip": scatter_chip,
+                    "sum": scatter_sum, "gain": gain_sum}[step]
+        note(when, only(where, action) if where else action, *args)
 
     def steps(kind):
         return [plan.get((kind, i), ()) for i in range(nblk)]
@@ -370,6 +460,12 @@
     pl.semaphore_wait(barrier, len(greet))
     send_own()
     for m in range(n):
+        if m == n - 1:
+            @pl.loop(0, nblk)
+            def _(i):
+                at_step(i, steps("p"))
+                partial(i)
+
         run(("s", m))
 
         @pl.loop(0, nblk)
@@ -384,12 +480,18 @@
             scatter_core()
 
     run(("s", n))
-
-    @pl.loop(0, nblk)
+    rest(0)
+
+    @pl.loop(1, nblk)
     def _(i):
-        at_step(i, steps(n))
-        results(i)
-
+        at_step(i, steps("f"))
+        copies = finish(i - 1)
+        rest(i)
+        for copy in copies:
+            copy.start()
+
+    for copy in finish(nblk - 1):
+        copy.start()
     run(("s", n + 1))
 
     for i in range(max(nblk - 2, 0), nblk):
@@ -403,11 +505,19 @@
     def sent(src, ssem):
         remote(src, src, ssem, ssem, partner).wait_send()
 
+    for way in range(2):
+        @pl.when(fits[way])
+        def _():
+            for e in range(2):
+                sent(spot(0, bx, by, c, e), s_z.at[way, e])
     for j in range(1, n):
         for e in range(2):
             here = spot(j, bx, by, c, e)
-            for sem in [s_z.at[j - 1, e], s_d.at[j - 1, e]]:
-                sent(here, sem)
+            sent(here, s_d.at[j - 1, e])
+            for way in range(2):
+                @pl.when(onward[j][way] == 1)
+                def _():
+                    sent(here, s_r.at[j - 1, e])
             for i in range(2):
                 sent(here, s_x.at[i, j - 1, e])
             for k in range(4):
@@ -503,6 +613,8 @@
             pltpu.VMEM((NB, s, WIN), BF),
             pltpu.VMEM((total, dim), BF),
             pltpu.VMEM((total, 3 * dim), BF),
+            pltpu.VMEM((total, dim), F32),
+            pltpu.VMEM((total, dim), F32),
             pltpu.VMEM((2, half, piece, dim), BF),
             pltpu.VMEM((half, piece, dim), BF),
             pltpu.VMEM((half - 1, piece, dim), BF),
@@ -517,6 +629,7 @@
             dma((2, nblk)),
             dma((2, 2)),
             dma((3,)),
+            dma((2, 2)),
             dma((n - 1, 2)),
             dma((n - 1, 2)),
             dma((2, n - 1, 2)),

time: 59.2 us -> 54.7 us (0.924)
  Pallas kernels: 58.4 us -> 53.7 us
    pallas_call x1, Pallas kernels: 54.7 us -> 50 us  [body(): pl.pallas_call(functools.partial(kernel, n, nd, s), out_shape=(jax.ShapeD...]
where the time goes in v3:
time: 54.7 us; the launch traced here: 54.5 us
  Pallas kernels  53.7 us (98%)
  between operations  0.8 us (1%)
    pallas_call x1, Pallas kernels, body(): pl.pallas_call(functools.partial(kernel, n, nd, s), out_shape=(jax.ShapeD...  50 us
    pallas_call x1, Pallas kernels, settle(): pl.pallas_call(functools.partial(settle_kernel, count), out_shape=tuple((...  3.64 us

profile of v3, /device:TPU:0, one launch (start us, length us, event | category | flops | bytes accessed | tf_op | source)
XLA Modules:
  0.0 54.5 jit_solution(10166621926008637375)
XLA Ops:
  0.6 50.0 %layer.1 = (bf16[1280,768]{1,0:T(8,128)(2,1)}, bf16[1280,768]{1,0:T(8,128)(2,1)}, f32[576,96]{1,0:T(8,128)}, f32[192,96]{1,0:T(8,128)}, f32[1,96]{1,0:T(1,128)}) custom-call(s32[16]{0:T(128)} %hist.1, bf16[1280,768]{1,0:T(8,128)(2,1)} %bitcast.13, bf16[1280,768]{1,0:T(8,128)(2,1)} %bitcast.14, f32[768]{0:T(1024)} %gain.1, bf16[576,768]{1,0:T(8,128)(2,1)} %bitcast.15, ...), custom_call_target="tpu_custom_call" | custom-call | tf_op jit(solution)/shard_map/layer/pallas_call | solution.py:583
  50.7 3.6 %settle.1 = (bf16[1280,768]{1,0:T(8,128)(2,1)}, bf16[1280,768]{1,0:T(8,128)(2,1)}, f32[576,96]{1,0:T(8,128)}, f32[192,96]{1,0:T(8,128)}, f32[1,96]{1,0:T(1,128)}) custom-call(bf16[1280,768]{1,0:T(8,128)(2,1)} %get-tuple-element.15.refs_0_, bf16[1280,768]{1,0:T(8,128)(2,1)} %get-tuple-element.16.refs_1_, f32[576,96]{1,0:T(8,128)} %get-tuple-element.17.refs_2_, ...), custom_call_target="tpu_custom_call" | custom-call | tf_op jit(solution)/shard_map/settle/pallas_call | solution.py:557

commit v4 on v3

--- a/solution.py
+++ b/solution.py
@@ -44,7 +44,7 @@
     (("p", 0), "c", 3, 0),
     (("p", 1), "c", 3, 1),
     (("s", 3), "d", 3),
-    (("f", 1), "sum"),
+    (("s", 4), "sum"),
     (("s", 5), "gain"),
 )
 BF = jnp.bfloat16
@@ -456,9 +456,9 @@
         for one in plan.get(when, ()):
             one()
 
-    prepare(0)
     pl.semaphore_wait(barrier, len(greet))
     send_own()
+    prepare(0)
     for m in range(n):
         if m == n - 1:
             @pl.loop(0, nblk)
@@ -551,7 +551,7 @@
 
 
 def settle(arrays):
-    count = 4
+    count = 8
     rows, dim = arrays[0].shape
     anywhere = pl.BlockSpec(memory_space=pl.ANY)
     return pl.pallas_call(

time: 54.7 us -> 55.3 us (1.011)
  Pallas kernels: 53.7 us -> 54.4 us
    pallas_call x1, Pallas kernels: 3.64 us -> 4.48 us  [settle(): pl.pallas_call(functools.partial(settle_kernel, count), out_shape=tuple((...]
where the time goes in v4:
time: 55.3 us; the launch traced here: 55.2 us
  Pallas kernels  54.4 us (98%)
  between operations  0.8 us (1%)
    pallas_call x1, Pallas kernels, body(): pl.pallas_call(functools.partial(kernel, n, nd, s), out_shape=(jax.ShapeD...  49.9 us
    pallas_call x1, Pallas kernels, settle(): pl.pallas_call(functools.partial(settle_kernel, count), out_shape=tuple((...  4.48 us

profile of v4, /device:TPU:0, one launch (start us, length us, event | category | flops | bytes accessed | tf_op | source)
XLA Modules:
  0.0 55.2 jit_solution(15849167747215555230)
XLA Ops:
  0.6 49.9 %layer.1 = (bf16[1280,768]{1,0:T(8,128)(2,1)}, bf16[1280,768]{1,0:T(8,128)(2,1)}, f32[576,96]{1,0:T(8,128)}, f32[192,96]{1,0:T(8,128)}, f32[1,96]{1,0:T(1,128)}) custom-call(s32[16]{0:T(128)} %hist.1, bf16[1280,768]{1,0:T(8,128)(2,1)} %bitcast.13, bf16[1280,768]{1,0:T(8,128)(2,1)} %bitcast.14, f32[768]{0:T(1024)} %gain.1, bf16[576,768]{1,0:T(8,128)(2,1)} %bitcast.15, ...), custom_call_target="tpu_custom_call" | custom-call | tf_op jit(solution)/shard_map/layer/pallas_call | solution.py:583
  50.5 4.5 %settle.1 = (bf16[1280,768]{1,0:T(8,128)(2,1)}, bf16[1280,768]{1,0:T(8,128)(2,1)}, f32[576,96]{1,0:T(8,128)}, f32[192,96]{1,0:T(8,128)}, f32[1,96]{1,0:T(1,128)}) custom-call(bf16[1280,768]{1,0:T(8,128)(2,1)} %get-tuple-element.15.refs_0_, bf16[1280,768]{1,0:T(8,128)(2,1)} %get-tuple-element.16.refs_1_, f32[576,96]{1,0:T(8,128)} %get-tuple-element.17.refs_2_, ...), custom_call_target="tpu_custom_call" | custom-call | tf_op jit(solution)/shard_map/settle/pallas_call | solution.py:557
